TPU v7x, 32 devices: a whole 2x2x4 slice. The times are simulated.
32 devices in a mesh: dp: 2 (over x), expert: 16 (over z, y, core).
Axes of the slice: x: 2, y: 2, z: 4, core: 2. Of those that a mesh axis runs over, the one named last changes fastest.
Arguments:
- tokens: bfloat16 [4096, 2048], P(('dp', 'expert')), may hold values from -6 to 6
- grad_out: bfloat16 [4096, 2048], P(('dp', 'expert')), may hold values from -0.125 to 0.125
- router_weight: bfloat16 [2048, 16], replicated, may hold values from -0.125 to 0.125
- expert_index: int32 [4096, 8], P(('dp', 'expert')), may hold values from 0 to 15, all different within a row; in each aligned block of 128 rows (0 to 127, 128 to 255, ...) at most 96 rows name the same one
- w_gate: bfloat16 [16, 2048, 768], P('expert'), may hold values from -0.125 to 0.125
- w_up: bfloat16 [16, 2048, 768], P('expert'), may hold values from -0.125 to 0.125
- w_down: bfloat16 [16, 768, 2048], P('expert'), may hold values from -0.21875 to 0.21875
Outputs:
- gate_grad: float32 [4096, 8], P(('dp', 'expert'))
- router_grad: float32 [2048, 16], P('expert')
Inputs may be any that keep to these rules, and one draw needn't show every extreme that they name: `expert_index`: each row names 8 different experts. In each aligned block of 128 rows (the rows of one device) no expert is named by more than 96 rows, a bound that some blocks reach.
All inputs are finite; a program needn't handle non-finite values.
Results may differ from a plain program's by a relative error of at most 0.009.
Values may be sent and summed in bfloat16 or wider, within the bound.
A program may use at most 128 MiB of HBM per device.

v0:
```python
import functools

import jax
import jax.numpy as jnp
from jax import lax
from jax.experimental import pallas as pl
from jax.experimental.pallas import tpu as pltpu
from jax.sharding import PartitionSpec as P


def plain(tokens, grad_out, router_weight, expert_index, w_gate, w_up, w_down):
    tok_rows, width = tokens.shape
    top = expert_index.shape[1]
    experts = router_weight.shape[1]
    me = lax.axis_index("expert")
    n = lax.axis_size("expert")
    index_all = lax.all_gather(expert_index, "expert", axis=0, tiled=True)
    tok_all = lax.all_gather(tokens, "expert", axis=0, tiled=True)
    grad_all = lax.all_gather(grad_out, "expert", axis=0, tiled=True)
    gate_in = jnp.dot(tok_all, w_gate[0], preferred_element_type=jnp.float32)
    up_in = jnp.dot(tok_all, w_up[0], preferred_element_type=jnp.float32)
    hidden = jax.nn.silu(gate_in) * up_in
    back = lax.dot_general(
        grad_all, w_down[0], (((1,), (1,)), ((), ())), preferred_element_type=jnp.float32
    )
    dots = jnp.sum(hidden * back, axis=1)
    dots_all = lax.all_gather(dots, "expert", axis=0).T
    labels = jnp.arange(experts, dtype=jnp.int32)
    picked = jnp.any(index_all[:, :, None] == labels, axis=1)
    logits = jnp.dot(tok_all, router_weight, preferred_element_type=jnp.float32)
    weights = jnp.where(picked, jnp.exp(jnp.where(picked, logits, 0.0)), 0.0)
    gates = weights / jnp.sum(weights, axis=1, keepdims=True)
    kept = jnp.where(picked, dots_all, 0.0)
    dense = gates * (kept - jnp.sum(gates * kept, axis=1, keepdims=True))
    cols = width // n
    mine = lax.dynamic_slice_in_dim(tok_all, me * cols, cols, axis=1)
    high = dense.astype(jnp.bfloat16)
    low = (dense - high.astype(jnp.float32)).astype(jnp.bfloat16)
    both = jnp.concatenate([high, low], axis=1)
    part = lax.dot_general(
        mine, both, (((0,), (0,)), ((), ())), preferred_element_type=jnp.float32
    )
    router_grad = lax.psum(part[:, :experts] + part[:, experts:], "dp")
    own = lax.dynamic_slice_in_dim(dots_all, me * tok_rows, tok_rows, axis=0)
    hits = (expert_index[:, :, None] == labels).astype(jnp.float32)
    gate_grad = jnp.sum(hits * own[:, None, :], axis=2)
    return (gate_grad, router_grad)


def layer_kernel(n, dp, tok_in, grad_in, rw_in, idx_in, wg_in, wu_in, wd_in, gg_out, rg_out,
                 tok, grad, idx, wg, wu, wd, hid, eo, lg, dots, part,
                 s_t, r_t, s_a, r_a, s_c, r_c, s_i, r_i, s_d, r_d, s_w, r_w, s_p, r_p, loc):
    plane = n // 2
    line = plane // 2
    me = lax.axis_index("expert")
    xd = lax.axis_index("dp")
    c = me % 2
    q = me // 2
    y = q % 2
    z = q // 2
    rows, width = tok_in.shape
    ff = wg_in.shape[2]
    experts, top = rw_in.shape[0], idx_in.shape[0]
    cut = rows * 5 // 8
    pair = 2 * rows

    def dev(zz, yy, cc):
        return {"expert": (zz * 2 + yy) * 2 + cc}

    def remote(src, dst, ss, rs, where):
        return pltpu.make_async_remote_copy(
            src_ref=src, dst_ref=dst, send_sem=ss, recv_sem=rs,
            device_id=where, device_id_type=pl.DeviceIdType.MESH)

    DOWN, UP, SIDE = 0, 1, 2

    def target(way):
        if way == DOWN:
            return dev(z - 1, y, c)
        if way == UP:
            return dev(z + 1, y, c)
        return dev(z, 1 - y, c)

    kinds = {"t": (tok, tok_in, 0, rows, s_t, r_t),
             "a": (grad, grad_in, 0, cut, s_a, r_a),
             "c": (grad, grad_in, cut, rows - cut, s_c, r_c)}

    def piece(kind, zb, yb, way, own=False):
        buf, inp, lo, size, ss, rs = kinds[kind]
        at = buf.at[zb, pl.ds(pl.multiple_of(yb * rows + lo, 16), size)]
        src = inp.at[pl.ds(lo, size)] if own else at
        return remote(src, at, ss.at[zb * 2 + yb, way], rs.at[zb * 2 + yb], target(way))

    def arrived(kind, zb, yb):
        piece(kind, zb, yb, SIDE).wait_recv()

    barrier = pltpu.get_barrier_semaphore()

    def plane_dev(k):
        return {"expert": ((q + k) % plane) * 2 + c}

    def owner_dev(k):
        return {"dp": (xd + k // 2) % dp, "expert": q * 2 + (c + k) % 2}

    for k in range(1, plane):
        pl.semaphore_signal(barrier, inc=1, device_id=plane_dev(k), device_id_type=pl.DeviceIdType.MESH)
    for k in range(1, 2 * dp):
        pl.semaphore_signal(barrier, inc=1, device_id=owner_dev(k), device_id_type=pl.DeviceIdType.MESH)
    mine = pl.ds(pl.multiple_of(y * rows, 16), rows)
    local = [pltpu.make_async_copy(tok_in, tok.at[z, mine], loc.at[0]),
             pltpu.make_async_copy(grad_in, grad.at[z, mine], loc.at[1]),
             pltpu.make_async_copy(idx_in, idx.at[q], loc.at[2]),
             pltpu.make_async_copy(wg_in.at[0], wg.at[c], loc.at[3]),
             pltpu.make_async_copy(wu_in.at[0], wu.at[c], loc.at[4]),
             pltpu.make_async_copy(wd_in.at[0], wd.at[c], loc.at[5])]
    for copy in local:
        copy.start()
    pl.semaphore_wait(barrier, plane - 1 + 2 * dp - 1)

    def own_z(kind, way):
        piece(kind, z, y, way, own=True).start()

    pl.when(z > 0)(lambda: own_z("t", DOWN))
    pl.when(z < line - 1)(lambda: own_z("t", UP))
    own_z("t", SIDE)
    other = {"expert": q * 2 + (1 - c)}
    weights = [remote(wg_in.at[0], wg.at[c], s_w.at[0], r_w.at[0], other),
               remote(wu_in.at[0], wu.at[c], s_w.at[1], r_w.at[1], other),
               remote(wd_in.at[0], wd.at[c], s_w.at[2], r_w.at[2], other)]
    for w in weights:
        w.start()
    index_sends = [remote(idx_in, idx.at[q], s_i.at[k], r_i.at[k], plane_dev(k)) for k in range(1, plane)]
    for w in index_sends:
        w.start()
    pl.when(z > 0)(lambda: own_z("a", DOWN))
    pl.when(z < line - 1)(lambda: own_z("a", UP))
    own_z("c", SIDE)

    def relay(kind, s):
        @pl.when(z + s < line)
        def _():
            arrived(kind, z + s, y)

            @pl.when(z > 0)
            def _():
                piece(kind, z + s, y, DOWN).start()
            piece(kind, z + s, y, SIDE).start()

        @pl.when(z - s >= 0)
        def _():
            arrived(kind, z - s, y)

            @pl.when(z < line - 1)
            def _():
                piece(kind, z - s, y, UP).start()
            piece(kind, z - s, y, SIDE).start()

    ft = ff // 3 if ff % 384 == 0 else ff
    dt = width // 4 if width % 512 == 0 else width

    def produce(zp):
        @pl.loop(0, 2)
        def _(r):
            @pl.loop(0, ff // ft)
            def _(j):
                at = pl.ds(pl.multiple_of(j * ft, 128), ft)
                x = tok[zp]
                g = jnp.dot(x, wg[r, :, at], preferred_element_type=jnp.float32)
                u = jnp.dot(x, wu[r, :, at], preferred_element_type=jnp.float32)
                hid[:, at] = (g / (1.0 + jnp.exp(-g)) * u).astype(jnp.bfloat16)

            @pl.loop(0, width // dt)
            def _(j):
                at = pl.ds(pl.multiple_of(j * dt, 128), dt)
                eo[zp, r, :, at] = jnp.dot(
                    hid[...], wd[r, :, at], preferred_element_type=jnp.float32).astype(jnp.bfloat16)
        lg[:, pl.ds(pl.multiple_of(zp * pair, 128), pair)] = lax.dot_general(
            rw_in[...], tok[zp], (((1,), (1,)), ((), ())), preferred_element_type=jnp.float32)

    def produce_ring(s):
        if s == 0:
            arrived("t", z, 1 - y)
            produce(z)
            return

        @pl.when(z + s < line)
        def _():
            arrived("t", z + s, 1 - y)
            produce(z + s)

        @pl.when(z - s >= 0)
        def _():
            arrived("t", z - s, 1 - y)
            produce(z - s)

    relay("t", 1)
    for copy in local:
        copy.wait()
    for w in weights:
        w.wait_recv()
    produce_ring(0)
    for s in range(2, line):
        relay("t", s)
    own_z("a", SIDE)
    arrived("c", z, 1 - y)
    for yb in range(2):
        pl.when(z > 0)(lambda yb=yb: piece("c", z, yb, DOWN).start())
        pl.when(z < line - 1)(lambda yb=yb: piece("c", z, yb, UP).start())

    for s in range(1, line):
        relay("a", s)
        produce_ring(s)

    def reduce_pair(zp):
        @pl.loop(0, 2)
        def _(r):
            total = jnp.zeros((pair, 128), jnp.float32)
            for j in range(width // 128):
                at = pl.ds(j * 128, 128)
                total += eo[zp, r, :, at].astype(jnp.float32) * grad[zp, :, at].astype(jnp.float32)
            row = jnp.sum(total.T, axis=0, keepdims=True)
            dots[q, pl.ds(r, 1), pl.ds(pl.multiple_of(zp * pair, 128), pair)] = row

    arrived("a", z, 1 - y)
    reduce_pair(z)
    for s in range(1, line):
        def take(zb, way, ok):
            for yb in range(2):
                arrived("c", zb, yb)
                pl.when(ok)(lambda yb=yb: piece("c", zb, yb, way).start())

        pl.when(z + s < line)(lambda: take(z + s, DOWN, z > 0))
        pl.when(z - s >= 0)(lambda: take(z - s, UP, z < line - 1))

        @pl.when(z + s < line)
        def _():
            arrived("a", z + s, 1 - y)
            reduce_pair(z + s)

        @pl.when(z - s >= 0)
        def _():
            arrived("a", z - s, 1 - y)
            reduce_pair(z - s)

    dot_sends = [remote(dots.at[q], dots.at[q], s_d.at[k], r_d.at[k], plane_dev(k)) for k in range(1, plane)]
    for w in dot_sends:
        w.start()
    for w in index_sends:
        w.wait()
    labels = lax.broadcasted_iota(jnp.int32, (experts, plane * rows), 0)
    chosen = jnp.zeros((experts, plane * rows), jnp.float32)
    for k in range(top):
        named = jnp.concatenate([idx[b, pl.ds(k, 1), :] for b in range(plane)], axis=1)
        chosen = jnp.where(labels == named, 1.0, chosen)
    weight = jnp.where(chosen > 0.0, jnp.exp(jnp.where(chosen > 0.0, lg[...], 0.0)), 0.0)
    gates = weight / jnp.sum(weight, axis=0, keepdims=True)
    for w in dot_sends:
        w.wait()
    all_dots = jnp.concatenate([dots[b] for b in range(plane)], axis=0)
    kept = jnp.where(chosen > 0.0, all_dots, 0.0)
    dense = gates * (kept - jnp.sum(gates * kept, axis=0, keepdims=True))
    high = dense.astype(jnp.bfloat16)
    low = (dense - high.astype(jnp.float32)).astype(jnp.bfloat16)
    cols = width // n
    at = pl.ds(pl.multiple_of(q * 2 * cols, 128), 2 * cols)
    both = jnp.concatenate([high, low], axis=0)
    split = jnp.zeros((2 * experts, 2 * cols), jnp.float32)
    for b in range(line):
        split += jnp.dot(both[:, b * pair:(b + 1) * pair], tok[b, :, at], preferred_element_type=jnp.float32)
    terms = split[:experts] + split[experts:]
    part[0, 0] = terms[:, :cols]
    part[0, 1] = terms[:, cols:]
    part_sends = [remote(part.at[0, (c + k) % 2], part.at[k, 0], s_p.at[k], r_p.at[k], owner_dev(k))
                  for k in range(1, 2 * dp)]
    for w in part_sends:
        w.start()
    own = jnp.concatenate(
        [dots[b, :, pl.ds(pl.multiple_of(q * rows, 128), rows)] for b in range(plane)], axis=0)
    names = idx[q]
    small = lax.broadcasted_iota(jnp.int32, (experts, rows), 0)
    for k in range(top):
        gg_out[pl.ds(k, 1), :] = jnp.sum(
            jnp.where(small == names[k:k + 1, :], own, 0.0), axis=0, keepdims=True)
    for w in part_sends:
        w.wait()
    total = part[0, c]
    for k in range(1, 2 * dp):
        total += part[k, 0]
    rg_out[...] = total

    for w in weights:
        w.wait_send()

    def gone(kind, zb, yb, way):
        piece(kind, zb, yb, way).wait_send()

    for kind in ("t", "a"):
        for zb in range(line):
            pl.when((zb >= z) & (z > 0))(lambda: gone(kind, zb, y, DOWN))
            pl.when((zb <= z) & (z < line - 1))(lambda: gone(kind, zb, y, UP))
            gone(kind, zb, y, SIDE)
    gone("c", z, y, SIDE)
    for zb in range(line):
        for yb in range(2):
            pl.when((zb >= z) & (z > 0))(lambda: gone("c", zb, yb, DOWN))
            pl.when((zb <= z) & (z < line - 1))(lambda: gone("c", zb, yb, UP))


def fused(n, dp, tokens, grad_out, router_weight, expert_index, w_gate, w_up, w_down):
    rows, width = tokens.shape
    ff = w_gate.shape[2]
    top = expert_index.shape[1]
    experts = router_weight.shape[1]
    plane, cols = n // 2, width // n
    line = plane // 2
    pair = 2 * rows
    anywhere = pl.BlockSpec(memory_space=pl.ANY)
    vmem = pl.BlockSpec(memory_space=pltpu.VMEM)
    dma = pltpu.SemaphoreType.DMA
    bf, f32 = jnp.bfloat16, jnp.float32
    gg, rg = pl.pallas_call(
        functools.partial(layer_kernel, n, dp),
        out_shape=(jax.ShapeDtypeStruct((top, rows), f32), jax.ShapeDtypeStruct((experts, cols), f32)),
        in_specs=[anywhere, anywhere, vmem, vmem, anywhere, anywhere, anywhere],
        out_specs=(vmem, vmem),
        scratch_shapes=[
            pltpu.VMEM((line, pair, width), bf),
            pltpu.VMEM((line, pair, width), bf),
            pltpu.VMEM((plane, top, rows), jnp.int32),
            pltpu.VMEM((2, width, ff), bf),
            pltpu.VMEM((2, width, ff), bf),
            pltpu.VMEM((2, ff, width), bf),
            pltpu.VMEM((pair, ff), bf),
            pltpu.VMEM((line, 2, pair, width), bf),
            pltpu.VMEM((experts, plane * rows), f32),
            pltpu.VMEM((plane, 2, plane * rows), f32),
            pltpu.VMEM((2 * dp, 2, experts, cols), f32),
            dma((plane, 3)), dma((plane,)), dma((plane, 3)), dma((plane,)), dma((plane, 3)), dma((plane,)),
            dma((plane,)), dma((plane,)), dma((plane,)), dma((plane,)),
            dma((3,)), dma((3,)), dma((2 * dp,)), dma((2 * dp,)), dma((6,)),
        ],
        compiler_params=pltpu.CompilerParams(
            collective_id=0, has_side_effects=True, vmem_limit_bytes=60 * 2**20),
    )(tokens, grad_out, router_weight.T, expert_index.T, w_gate, w_up, w_down)
    return gg.T, rg.T


def solution(mesh):
    n, dp = mesh.shape["expert"], mesh.shape["dp"]

    def on_device(tokens, grad_out, router_weight, expert_index, w_gate, w_up, w_down):
        rows, width = tokens.shape
        ff = w_gate.shape[2]
        held = 2 * (2 * n // 2 * rows * width * 2 + 6 * ff * width)
        fits = n % 4 == 0 and n >= 8 and held < 44 * 2**20 and width % (128 * n) == 0
        fits = fits and rows % 128 == 0 and router_weight.shape[1] == n
        body = functools.partial(fused, n, dp) if fits else plain
        return body(tokens, grad_out, router_weight, expert_index, w_gate, w_up, w_down)

    in_specs = (
        P(("dp", "expert"), None),
        P(("dp", "expert"), None),
        P(),
        P(("dp", "expert"), None),
        P("expert", None, None),
        P("expert", None, None),
        P("expert", None, None),
    )
    out_specs = (P(("dp", "expert"), None), P("expert", None))
    return jax.shard_map(
        on_device, mesh=mesh, in_specs=in_specs, out_specs=out_specs, check_vma=False
    )
```

profile of v0, /device:TPU:0, one launch (start us, length us, event | category | flops | bytes accessed | tf_op | source)
XLA Modules:
  0.0 103.5 jit_solution(848484901015747526)
XLA Ops:
  0.6 100.3 %shard_map.86 = (f32[8,128]{1,0:T(8,128)}, f32[16,128]{1,0:T(8,128)}) custom-call(bf16[128,2048]{1,0:T(8,128)(2,1)} %tok_in.1, bf16[128,2048]{1,0:T(8,128)(2,1)} %grad_in.1, bf16[16,2048]{1,0:T(8,128)(2,1)} %bitcast.4, s32[8,128]{1,0:T(8,128)} %bitcast.6, bf16[1,2048,768]{2,1,0:T(8,128)(2,1)} %wg_in.1, bf16[1,2048,768]{2,1,0:T(8,128)(2,1)} %wu_in.1, ...), custom_call_target="tpu_custom_call" | custom-call | tf_op jit(solution)/shard_map/pallas_call | solution.py:321
  100.9 1.3 %copy.11 = f32[128,8]{0,1:T(8,128)} copy(f32[128,8]{0,1:T(8,128)} %bitcast.7) | data formatting | bytes 8192
  102.2 1.3 %copy.12 = f32[128,16]{0,1:T(8,128)} copy(f32[128,16]{0,1:T(8,128)} %bitcast.5) | data formatting | bytes 16384
where the time goes:
time: 104 us; the launch traced here: 103 us
  Pallas kernels  100 us (96%)
  local copies, waits for them, and re-layouts  2.56 us (2%)
    pallas_call x1, Pallas kernels, fused(): pl.pallas_call(functools.partial(layer_kernel, n, dp), out_shape=(jax.Sha...  100 us
    unnamed x2, local copies, waits for them, and re-layouts  2.56 us

commit v1 on v0

--- a/solution.py
+++ b/solution.py
@@ -48,7 +48,7 @@
 
 
 def layer_kernel(n, dp, tok_in, grad_in, rw_in, idx_in, wg_in, wu_in, wd_in, gg_out, rg_out,
-                 tok, grad, idx, wg, wu, wd, hid, eo, lg, dots, part,
+                 tok, grad, rw, idx, wg, wu, wd, hid, eo, lg, dots, part,
                  s_t, r_t, s_a, r_a, s_c, r_c, s_i, r_i, s_d, r_d, s_w, r_w, s_p, r_p, loc):
     plane = n // 2
     line = plane // 2
@@ -102,8 +102,12 @@
     def owner_dev(k):
         return {"dp": (xd + k // 2) % dp, "expert": q * 2 + (c + k) % 2}
 
-    for k in range(1, plane):
-        pl.semaphore_signal(barrier, inc=1, device_id=plane_dev(k), device_id_type=pl.DeviceIdType.MESH)
+    def greet(where):
+        pl.semaphore_signal(barrier, inc=1, device_id=where, device_id_type=pl.DeviceIdType.MESH)
+
+    pl.when(z > 0)(lambda: greet(target(DOWN)))
+    pl.when(z < line - 1)(lambda: greet(target(UP)))
+    greet(target(SIDE))
     for k in range(1, 2 * dp):
         pl.semaphore_signal(barrier, inc=1, device_id=owner_dev(k), device_id_type=pl.DeviceIdType.MESH)
     mine = pl.ds(pl.multiple_of(y * rows, 16), rows)
@@ -112,10 +116,12 @@
              pltpu.make_async_copy(idx_in, idx.at[q], loc.at[2]),
              pltpu.make_async_copy(wg_in.at[0], wg.at[c], loc.at[3]),
              pltpu.make_async_copy(wu_in.at[0], wu.at[c], loc.at[4]),
-             pltpu.make_async_copy(wd_in.at[0], wd.at[c], loc.at[5])]
+             pltpu.make_async_copy(wd_in.at[0], wd.at[c], loc.at[5]),
+             pltpu.make_async_copy(rw_in, rw, loc.at[6])]
     for copy in local:
         copy.start()
-    pl.semaphore_wait(barrier, plane - 1 + 2 * dp - 1)
+    pl.when((z > 0) & (z < line - 1))(lambda: pl.semaphore_wait(barrier, 2 + 2 * dp))
+    pl.when((z == 0) | (z == line - 1))(lambda: pl.semaphore_wait(barrier, 1 + 2 * dp))
 
     def own_z(kind, way):
         piece(kind, z, y, way, own=True).start()
@@ -130,8 +136,6 @@
     for w in weights:
         w.start()
     index_sends = [remote(idx_in, idx.at[q], s_i.at[k], r_i.at[k], plane_dev(k)) for k in range(1, plane)]
-    for w in index_sends:
-        w.start()
     pl.when(z > 0)(lambda: own_z("a", DOWN))
     pl.when(z < line - 1)(lambda: own_z("a", UP))
     own_z("c", SIDE)
@@ -175,7 +179,7 @@
                 eo[zp, r, :, at] = jnp.dot(
                     hid[...], wd[r, :, at], preferred_element_type=jnp.float32).astype(jnp.bfloat16)
         lg[:, pl.ds(pl.multiple_of(zp * pair, 128), pair)] = lax.dot_general(
-            rw_in[...], tok[zp], (((1,), (1,)), ((), ())), preferred_element_type=jnp.float32)
+            rw[...], tok[zp], (((1,), (1,)), ((), ())), preferred_element_type=jnp.float32)
 
     def produce_ring(s):
         if s == 0:
@@ -210,6 +214,9 @@
     for s in range(1, line):
         relay("a", s)
         produce_ring(s)
+
+    for w in index_sends:
+        w.start()
 
     def reduce_pair(zp):
         @pl.loop(0, 2)
@@ -320,12 +327,13 @@
     bf, f32 = jnp.bfloat16, jnp.float32
     gg, rg = pl.pallas_call(
         functools.partial(layer_kernel, n, dp),
-        out_shape=(jax.ShapeDtypeStruct((top, rows), f32), jax.ShapeDtypeStruct((experts, cols), f32)),
-        in_specs=[anywhere, anywhere, vmem, vmem, anywhere, anywhere, anywhere],
+        out_shape=(pltpu.VMEM((top, rows), f32), pltpu.VMEM((experts, cols), f32)),
+        in_specs=[anywhere] * 7,
         out_specs=(vmem, vmem),
         scratch_shapes=[
             pltpu.VMEM((line, pair, width), bf),
             pltpu.VMEM((line, pair, width), bf),
+            pltpu.VMEM((experts, width), bf),
             pltpu.VMEM((plane, top, rows), jnp.int32),
             pltpu.VMEM((2, width, ff), bf),
             pltpu.VMEM((2, width, ff), bf),
@@ -337,11 +345,22 @@
             pltpu.VMEM((2 * dp, 2, experts, cols), f32),
             dma((plane, 3)), dma((plane,)), dma((plane, 3)), dma((plane,)), dma((plane, 3)), dma((plane,)),
             dma((plane,)), dma((plane,)), dma((plane,)), dma((plane,)),
-            dma((3,)), dma((3,)), dma((2 * dp,)), dma((2 * dp,)), dma((6,)),
+            dma((3,)), dma((3,)), dma((2 * dp,)), dma((2 * dp,)), dma((7,)),
         ],
         compiler_params=pltpu.CompilerParams(
             collective_id=0, has_side_effects=True, vmem_limit_bytes=60 * 2**20),
     )(tokens, grad_out, router_weight.T, expert_index.T, w_gate, w_up, w_down)
+    def finish(a, b, x, y):
+        x[...] = a[...]
+        y[...] = b[...]
+    gg = pltpu.with_memory_space_constraint(gg, pltpu.VMEM)
+    rg = pltpu.with_memory_space_constraint(rg, pltpu.VMEM)
+    gg, rg = pl.pallas_call(
+        finish,
+        out_shape=(jax.ShapeDtypeStruct((top, rows), f32), jax.ShapeDtypeStruct((experts, cols), f32)),
+        in_specs=[vmem, vmem],
+        out_specs=(vmem, vmem),
+    )(gg, rg)
     return gg.T, rg.T
 
 

time: 104 us -> 98.6 us (0.948)
  local copies, waits for them, and re-layouts: 2.56 us -> 0 us
  Pallas kernels: 100 us -> 97.8 us
    unnamed x2 -> x0, local copies, waits for them, and re-layouts: 2.56 us -> none
    pallas_call x1 -> x2, Pallas kernels: 100 us -> 97.8 us  [the longest x1 97.2 us: fused(): pl.pallas_call(functools.partial(layer_kernel, n, dp), out_shape=(pltpu.V...]
where the time goes in v1:
time: 98.6 us; the launch traced here: 98.4 us
  Pallas kernels  97.8 us (99%)
    pallas_call x1, Pallas kernels, fused(): pl.pallas_call(functools.partial(layer_kernel, n, dp), out_shape=(pltpu.V...  97.2 us

profile of v1, /device:TPU:0, one launch (start us, length us, event | category | flops | bytes accessed | tf_op | source)
XLA Modules:
  0.0 98.4 jit_solution(1275692827165206879)
XLA Ops:
  0.6 97.2 %shard_map.86 = (f32[8,128]{1,0:T(8,128)S(1)}, f32[16,128]{1,0:T(8,128)S(1)}) custom-call(bf16[128,2048]{1,0:T(8,128)(2,1)} %tok_in.1, bf16[128,2048]{1,0:T(8,128)(2,1)} %grad_in.1, bf16[16,2048]{1,0:T(8,128)(2,1)} %bitcast.4, s32[8,128]{1,0:T(8,128)} %bitcast.5, bf16[1,2048,768]{2,1,0:T(8,128)(2,1)} %wg_in.1, bf16[1,2048,768]{2,1,0:T(8,128)(2,1)} %wu_in.1, ...), custom_call_target="tpu_custom_call" | custom-call | tf_op jit(solution)/shard_map/pallas_call | solution.py:328
  97.8 0.6 shard_map.87

commit v2 on v1

v2 whole, which is shorter than its diff:
```python
import functools

import jax
import jax.numpy as jnp
from jax import lax
from jax.experimental import pallas as pl
from jax.experimental.pallas import tpu as pltpu
from jax.sharding import PartitionSpec as P


def plain(tokens, grad_out, router_weight, expert_index, w_gate, w_up, w_down):
    tok_rows, width = tokens.shape
    top = expert_index.shape[1]
    experts = router_weight.shape[1]
    me = lax.axis_index("expert")
    n = lax.axis_size("expert")
    index_all = lax.all_gather(expert_index, "expert", axis=0, tiled=True)
    tok_all = lax.all_gather(tokens, "expert", axis=0, tiled=True)
    grad_all = lax.all_gather(grad_out, "expert", axis=0, tiled=True)
    gate_in = jnp.dot(tok_all, w_gate[0], preferred_element_type=jnp.float32)
    up_in = jnp.dot(tok_all, w_up[0], preferred_element_type=jnp.float32)
    hidden = jax.nn.silu(gate_in) * up_in
    back = lax.dot_general(
        grad_all, w_down[0], (((1,), (1,)), ((), ())), preferred_element_type=jnp.float32
    )
    dots = jnp.sum(hidden * back, axis=1)
    dots_all = lax.all_gather(dots, "expert", axis=0).T
    labels = jnp.arange(experts, dtype=jnp.int32)
    picked = jnp.any(index_all[:, :, None] == labels, axis=1)
    logits = jnp.dot(tok_all, router_weight, preferred_element_type=jnp.float32)
    weights = jnp.where(picked, jnp.exp(jnp.where(picked, logits, 0.0)), 0.0)
    gates = weights / jnp.sum(weights, axis=1, keepdims=True)
    kept = jnp.where(picked, dots_all, 0.0)
    dense = gates * (kept - jnp.sum(gates * kept, axis=1, keepdims=True))
    cols = width // n
    mine = lax.dynamic_slice_in_dim(tok_all, me * cols, cols, axis=1)
    high = dense.astype(jnp.bfloat16)
    low = (dense - high.astype(jnp.float32)).astype(jnp.bfloat16)
    both = jnp.concatenate([high, low], axis=1)
    part = lax.dot_general(
        mine, both, (((0,), (0,)), ((), ())), preferred_element_type=jnp.float32
    )
    router_grad = lax.psum(part[:, :experts] + part[:, experts:], "dp")
    own = lax.dynamic_slice_in_dim(dots_all, me * tok_rows, tok_rows, axis=0)
    hits = (expert_index[:, :, None] == labels).astype(jnp.float32)
    gate_grad = jnp.sum(hits * own[:, None, :], axis=2)
    return (gate_grad, router_grad)


OUT, IN, SIDE = 0, 1, 2

END = {
    "start": [("S", "x", 3, 0, 0, IN, SIDE), ("S", "x", 3, 0, 1, IN, SIDE),
              ("S", "g", 3, 0, 0, IN), ("S", "g", 3, 0, 1, IN), ("send_down",)],
    "p0": [("F", "x", 2, 0, 0, SIDE), ("F", "x", 2, 0, 1, SIDE), ("W", "x", 3, 1, 0), ("W", "x", 3, 1, 1)],
    "p1": [("F", "x", 1, 0, 0, SIDE)],
    "p2": [("send_hidden",), ("F", "x", 1, 0, 1, SIDE), ("W", "x", 2, 1, 0), ("W", "x", 2, 1, 1)],
    "p3": [("F", "x", 0, 0, 0, SIDE)],
    "p4": [("F", "x", 0, 0, 1, SIDE), ("W", "x", 1, 1, 0), ("W", "x", 1, 1, 1)],
    "p5": [("F", "g", 2, 0, 1, SIDE)],
    "p6": [("F", "g", 1, 0, 0, SIDE), ("W", "x", 0, 1, 0), ("W", "x", 0, 1, 1)],
    "p7": [],
    "r0": [("F", "g", 1, 0, 1, SIDE)],
    "r1": [("F", "g", 0, 0, 0, SIDE)],
    "r2": [("F", "g", 0, 0, 1, SIDE)],
    "r3": [("W", "g", 1, 1, 0), ("W", "g", 1, 1, 1)],
    "r4": [("W", "g", 2, 0, 0)],
    "r5": [("W", "g", 2, 1, 1), ("W", "g", 2, 1, 0)],
    "r6": [("W", "g", 0, 1, 0), ("W", "g", 0, 1, 1)],
    "r7": [],
}
NEXT = {
    "start": [("S", "x", 2, 0, 0, OUT, IN, SIDE), ("S", "x", 2, 0, 1, OUT, IN, SIDE)],
    "p0": [("F", "x", 3, 0, 0, IN, SIDE), ("F", "x", 1, 0, 0, OUT, SIDE),
           ("F", "x", 3, 0, 1, IN, SIDE), ("F", "x", 1, 0, 1, OUT, SIDE),
           ("S", "g", 2, 0, 0, IN, SIDE), ("W", "x", 2, 1, 0), ("W", "x", 2, 1, 1)],
    "p1": [("F", "x", 0, 0, 0, OUT, SIDE), ("F", "g", 3, 0, 0, IN, SIDE)],
    "p2": [("F", "x", 0, 0, 1, OUT, SIDE), ("F", "g", 3, 0, 1, IN, SIDE), ("S", "g", 2, 0, 1, OUT, IN, SIDE),
           ("W", "x", 3, 1, 0), ("W", "x", 3, 1, 1)],
    "p3": [("F", "g", 1, 0, 0, OUT), ("pass_down", 0)],
    "p4": [("W", "x", 1, 1, 0), ("W", "x", 1, 1, 1)],
    "p5": [("pass_down", 1), ("F", "g", 2, 1, 0, IN)],
    "p6": [("F", "g", 1, 0, 1, OUT, SIDE), ("cross_down", 0), ("F", "g", 0, 0, 0, OUT), ("pass_down", 2),
           ("F", "g", 3, 1, 0, IN), ("cross_down", 1), ("F", "g", 0, 0, 1, OUT), ("S", "g", 2, 0, 0, OUT),
           ("P", "g", 2, 1, 0, OUT), ("W", "x", 0, 1, 0), ("W", "x", 0, 1, 1)],
    "p7": [("pass_down", 3), ("cross_down", 2)],
    "r0": [("F", "g", 3, 1, 1, IN)],
    "r1": [],
    "r2": [],
    "r3": [("cross_down", 3)],
    "r4": [("help",)],
    "r5": [("W", "g", 0, 1, 0), ("W", "g", 0, 1, 1)],
    "r6": [("W", "g", 2, 1, 1)],
    "r7": [("W", "g", 1, 1, 0), ("W", "g", 1, 1, 1)],
}
BLOCKS = [((3, 0), (2, 0)), ((1, 0), (3, 0)), ((0, 0), (1, 0)), ((1, 1), (0, 0)),
          ((2, 0), (3, 1)), ((2, 1), (0, 1)), ((0, 1), (2, 1)), ((0, 1), (1, 1))]
CHUNKS = 4


def layer_kernel(n, dp, tok_in, grad_in, rw_in, idx_in, wg_in, wu_in, wd_in, gg_out, rg_out,
                 tok, grad, rw, idx, wg, wu, wd, hid, eo, lg, dots, part, far_wd, sent, extra,
                 s_x, r_x, s_g, r_g, s_i, r_i, s_d, r_d, s_w, r_w, s_p, r_p, s_e, r_e,
                 s_f, r_f, s_fx, r_fx, s_fc, r_fc, s_h, r_h, loc):
    plane = n // 2
    line = plane // 2
    me = lax.axis_index("expert")
    xd = lax.axis_index("dp")
    c = me % 2
    q = me // 2
    y = q % 2
    z = q // 2
    rows, width = tok_in.shape
    ff = wg_in.shape[2]
    experts, top = rw_in.shape[0], idx_in.shape[0]
    pair = 2 * rows
    half = rows // 2
    upper = z // (line // 2)
    own = upper * z + (1 - upper) * (line - 1 - z)
    end = own - (line - 2)
    step = 2 * upper - 1

    def real(m):
        return upper * m + (1 - upper) * (line - 1 - m)

    def side(f):
        return y + f - 2 * y * f

    def dev(zz, yy, cc):
        return {"expert": (zz * 2 + yy) * 2 + cc}

    def remote(src, dst, ss, rs, where):
        return pltpu.make_async_remote_copy(
            src_ref=src, dst_ref=dst, send_sem=ss, recv_sem=rs,
            device_id=where, device_id_type=pl.DeviceIdType.MESH)

    def target(way):
        if way == OUT:
            return dev(z + step, y, c)
        if way == IN:
            return dev(z - step, y, c)
        return dev(z, 1 - y, c)

    kinds = {"x": (tok, tok_in, s_x, r_x), "g": (grad, grad_in, s_g, r_g)}

    def piece(kind, m, f, part_of, way, mine=False):
        buf, inp, ss, rs = kinds[kind]
        zb, yb = real(m), side(f)
        at = buf.at[zb, pl.ds(pl.multiple_of(yb * rows + part_of * half, 16), half)]
        src = inp.at[pl.ds(part_of * half, half)] if mine else at
        slot = (zb * 2 + yb) * 2 + part_of
        return remote(src, at, ss.at[slot, way], rs.at[slot], target(way))

    twin = {"dp": (xd + 1) % dp}
    mate = {"expert": q * 2 + (1 - c)}

    def down_rows(which, k):
        size = ff // dp // CHUNKS
        return pl.ds(pl.multiple_of(which * (ff // dp) + k * size, 16), size)

    def down(k):
        at = down_rows(xd, k)
        return remote(wd_in.at[0, at], far_wd.at[c, at], s_f.at[k], r_f.at[k], target(IN))

    def down_twin(k):
        at = far_wd.at[c, down_rows(xd, k)]
        return remote(at, at, s_fx.at[k], r_fx.at[k], twin)

    def down_mate(other, k):
        at = far_wd.at[c, down_rows((xd + other) % dp, k)]
        return remote(at, at, s_fc.at[other * CHUNKS + k], r_fc.at[other * CHUNKS + k], mate)

    def hidden_send():
        return remote(sent, sent, s_h.at[0], r_h.at[0], target(IN))

    def plane_dev(k):
        return {"expert": ((q + k) % plane) * 2 + c}

    def owner_dev(k):
        return {"dp": (xd + k // 2) % dp, "expert": q * 2 + (c + k) % 2}

    at_end = real(line - 1) * 2 + y
    extra_sends = [remote(extra.at[at_end], extra.at[at_end], s_e.at[k], r_e.at[at_end], plane_dev(k))
                   for k in range(1, plane)]

    def block_dots(left, right):
        total = jnp.zeros((rows, 128), jnp.float32)
        for j in range(width // 128):
            total += left(j).astype(jnp.float32) * right(j).astype(jnp.float32)
        return jnp.sum(total.T, axis=0, keepdims=True)

    dt = width // 4 if width % 512 == 0 else width

    def help_end():
        hidden_send().wait_recv()
        for k in range(CHUNKS):
            down_mate(0, k).wait_recv()
            down_mate(1, k).wait_recv()
        theirs = pl.ds(pl.multiple_of((1 - y) * rows, 16), rows)

        @pl.loop(0, 2)
        def _(r):
            total = jnp.zeros((rows, 128), jnp.float32)
            for j in range(width // dt):
                got = jnp.dot(sent[r], far_wd[r, :, j * dt:(j + 1) * dt],
                              preferred_element_type=jnp.float32).astype(jnp.bfloat16).astype(jnp.float32)
                for i in range(dt // 128):
                    lo = j * dt + i * 128
                    total += got[:, i * 128:(i + 1) * 128] * grad[
                        real(line - 1), theirs, lo:lo + 128].astype(jnp.float32)
            extra[at_end, pl.ds(r, 1), :] = jnp.sum(total.T, axis=0, keepdims=True)
        for w in extra_sends:
            w.start()

    def run(ops):
        for op in ops:
            if op[0] == "send_down":
                for k in range(CHUNKS):
                    down(k).start()
            elif op[0] == "send_hidden":
                hidden_send().start()
            elif op[0] == "pass_down":
                down(op[1]).wait_recv()
                down_twin(op[1]).start()
                down_mate(0, op[1]).start()
            elif op[0] == "cross_down":
                down_twin(op[1]).wait_recv()
                down_mate(1, op[1]).start()
            elif op[0] == "help":
                help_end()
            else:
                what, kind, m, f, part_of = op[:5]
                if what in "FW":
                    piece(kind, m, f, part_of, SIDE).wait_recv()
                for way in op[5:]:
                    piece(kind, m, f, part_of, way, mine=what == "S").start()

    def slot(name):
        if END[name]:
            pl.when(end == 1)(lambda: run(END[name]))
        if NEXT[name]:
            pl.when(end == 0)(lambda: run(NEXT[name]))

    def sent_all(table):
        for ops in table.values():
            for op in ops:
                if op[0] == "send_down":
                    for k in range(CHUNKS):
                        down(k).wait_send()
                elif op[0] == "send_hidden":
                    hidden_send().wait_send()
                elif op[0] == "pass_down":
                    down_twin(op[1]).wait_send()
                    down_mate(0, op[1]).wait_send()
                elif op[0] == "cross_down":
                    down_mate(1, op[1]).wait_send()
                elif op[0] == "help":
                    for w in extra_sends:
                        w.wait_send()
                else:
                    for way in op[5:]:
                        piece(op[1], op[2], op[3], op[4], way).wait_send()

    barrier = pltpu.get_barrier_semaphore()

    def greet(where):
        pl.semaphore_signal(barrier, inc=1, device_id=where, device_id_type=pl.DeviceIdType.MESH)

    pl.when(end == 0)(lambda: greet(target(OUT)))
    greet(target(IN))
    greet(target(SIDE))
    for k in range(1, 2 * dp):
        greet(owner_dev(k))
    mine = pl.ds(pl.multiple_of(y * rows, 16), rows)
    local = [pltpu.make_async_copy(tok_in, tok.at[z, mine], loc.at[0]),
             pltpu.make_async_copy(grad_in, grad.at[z, mine], loc.at[1]),
             pltpu.make_async_copy(idx_in, idx.at[q], loc.at[2]),
             pltpu.make_async_copy(wg_in.at[0], wg.at[c], loc.at[3]),
             pltpu.make_async_copy(wu_in.at[0], wu.at[c], loc.at[4]),
             pltpu.make_async_copy(wd_in.at[0], wd.at[c], loc.at[5]),
             pltpu.make_async_copy(rw_in, rw, loc.at[6])]
    for copy in local:
        copy.start()
    pl.when(end == 0)(lambda: pl.semaphore_wait(barrier, 2 + 2 * dp))
    pl.when(end == 1)(lambda: pl.semaphore_wait(barrier, 1 + 2 * dp))

    slot("start")
    weights = [remote(wg_in.at[0], wg.at[c], s_w.at[0], r_w.at[0], mate),
               remote(wu_in.at[0], wu.at[c], s_w.at[1], r_w.at[1], mate),
               remote(wd_in.at[0], wd.at[c], s_w.at[2], r_w.at[2], mate)]
    for w in weights:
        w.start()
    index_sends = [remote(idx_in, idx.at[q], s_i.at[k], r_i.at[k], plane_dev(k)) for k in range(1, plane)]

    ft = ff // 3 if ff % 384 == 0 else ff

    def produce(zp, r, first, keep):
        @pl.loop(0, ff // ft)
        def _(j):
            at = pl.ds(pl.multiple_of(j * ft, 128), ft)
            x = tok[zp]
            g = jnp.dot(x, wg[r, :, at], preferred_element_type=jnp.float32)
            u = jnp.dot(x, wu[r, :, at], preferred_element_type=jnp.float32)
            hid[:, at] = (g / (1.0 + jnp.exp(-g)) * u).astype(jnp.bfloat16)

        if keep:
            @pl.when(end == 1)
            def _():
                sent[r] = hid[pl.ds(pl.multiple_of((1 - y) * rows, 16), rows), :]

        @pl.loop(0, width // dt)
        def _(j):
            at = pl.ds(pl.multiple_of(j * dt, 128), dt)
            eo[zp, r, :, at] = jnp.dot(
                hid[...], wd[r, :, at], preferred_element_type=jnp.float32).astype(jnp.bfloat16)
        if first:
            lg[:, pl.ds(pl.multiple_of(zp * pair, 128), pair)] = lax.dot_general(
                rw[...], tok[zp], (((1,), (1,)), ((), ())), preferred_element_type=jnp.float32)

    order = [2 + end, 3 - end, 1, 0]
    for i in range(line):
        for k in range(2):
            slot("p" + str(2 * i + k))
            if i == 0 and k == 0:
                for copy in local:
                    copy.wait()
            if i == 0 and k == 1:
                for w in weights:
                    w.wait_recv()
            produce(real(order[i]), c + k - 2 * c * k, k == 0, i == 0)

    for w in index_sends:
        w.start()

    def reduce_block(zb, yb):
        at = pl.ds(pl.multiple_of(yb * rows, 16), rows)

        @pl.loop(0, 2)
        def _(r):
            row = block_dots(lambda j: eo[zb, r, at, j * 128:(j + 1) * 128],
                             lambda j: grad[zb, at, j * 128:(j + 1) * 128])
            dots[q, zb * 2 + yb, pl.ds(r, 1), :] = row

    for i, (a, b) in enumerate(BLOCKS):
        slot("r" + str(i))
        m = end * a[0] + (1 - end) * b[0]
        f = end * a[1] + (1 - end) * b[1]
        if i < len(BLOCKS) - 1:
            reduce_block(real(m), side(f))
        else:
            pl.when(end == 0)(lambda: reduce_block(real(m), side(f)))

    dot_sends = [remote(dots.at[q], dots.at[q], s_d.at[k], r_d.at[k], plane_dev(k)) for k in range(1, plane)]
    for w in dot_sends:
        w.start()
    for w in index_sends:
        w.wait()
    labels = lax.broadcasted_iota(jnp.int32, (experts, plane * rows), 0)
    chosen = jnp.zeros((experts, plane * rows), jnp.float32)
    for k in range(top):
        named = jnp.concatenate([idx[b, pl.ds(k, 1), :] for b in range(plane)], axis=1)
        chosen = jnp.where(labels == named, 1.0, chosen)
    weight = jnp.where(chosen > 0.0, jnp.exp(jnp.where(chosen > 0.0, lg[...], 0.0)), 0.0)
    gates = weight / jnp.sum(weight, axis=0, keepdims=True)
    ends = {0: 2, 1: 3, plane - 2: plane - 4, plane - 1: plane - 3}
    for b, helper in ends.items():
        pl.when(q != helper)(lambda: remote(
            extra.at[b], extra.at[b], s_e.at[1], r_e.at[b], plane_dev(1)).wait_recv())
    for w in dot_sends:
        w.wait()

    def dots_of(b):
        blocks = [dots[b, k] for k in range(plane)]
        if b in ends:
            blocks[b ^ 1] = extra[b]
        return jnp.concatenate(blocks, axis=1)

    all_dots = jnp.concatenate([dots_of(b) for b in range(plane)], axis=0)
    kept = jnp.where(chosen > 0.0, all_dots, 0.0)
    dense = gates * (kept - jnp.sum(gates * kept, axis=0, keepdims=True))
    high = dense.astype(jnp.bfloat16)
    low = (dense - high.astype(jnp.float32)).astype(jnp.bfloat16)
    cols = width // n
    at = pl.ds(pl.multiple_of(q * 2 * cols, 128), 2 * cols)
    both = jnp.concatenate([high, low], axis=0)
    split = jnp.zeros((2 * experts, 2 * cols), jnp.float32)
    for b in range(line):
        split += jnp.dot(both[:, b * pair:(b + 1) * pair], tok[b, :, at], preferred_element_type=jnp.float32)
    terms = split[:experts] + split[experts:]
    part[0, 0] = terms[:, :cols]
    part[0, 1] = terms[:, cols:]
    part_sends = [remote(part.at[0, (c + k) % 2], part.at[k, 0], s_p.at[k], r_p.at[k], owner_dev(k))
                  for k in range(1, 2 * dp)]
    for w in part_sends:
        w.start()
    held = [jnp.where(q == (b ^ 1), extra[b], dots[b, q]) if b in ends else dots[b, q] for b in range(plane)]
    held = jnp.concatenate(held, axis=0)
    names = idx[q]
    small = lax.broadcasted_iota(jnp.int32, (experts, rows), 0)
    for k in range(top):
        gg_out[pl.ds(k, 1), :] = jnp.sum(
            jnp.where(small == names[k:k + 1, :], held, 0.0), axis=0, keepdims=True)
    for w in weights:
        w.wait_send()
    pl.when(end == 1)(lambda: sent_all(END))
    pl.when(end == 0)(lambda: sent_all(NEXT))
    for w in part_sends:
        w.wait()
    total = part[0, c]
    for k in range(1, 2 * dp):
        total += part[k, 0]
    rg_out[...] = total


def fused(n, dp, tokens, grad_out, router_weight, expert_index, w_gate, w_up, w_down):
    rows, width = tokens.shape
    ff = w_gate.shape[2]
    top = expert_index.shape[1]
    experts = router_weight.shape[1]
    plane, cols = n // 2, width // n
    line = plane // 2
    pair = 2 * rows
    anywhere = pl.BlockSpec(memory_space=pl.ANY)
    vmem = pl.BlockSpec(memory_space=pltpu.VMEM)
    dma = pltpu.SemaphoreType.DMA
    bf, f32 = jnp.bfloat16, jnp.float32
    gg, rg = pl.pallas_call(
        functools.partial(layer_kernel, n, dp),
        out_shape=(pltpu.VMEM((top, rows), f32), pltpu.VMEM((experts, cols), f32)),
        in_specs=[anywhere] * 7,
        out_specs=(vmem, vmem),
        scratch_shapes=[
            pltpu.VMEM((line, pair, width), bf),
            pltpu.VMEM((line, pair, width), bf),
            pltpu.VMEM((experts, width), bf),
            pltpu.VMEM((plane, top, rows), jnp.int32),
            pltpu.VMEM((2, width, ff), bf),
            pltpu.VMEM((2, width, ff), bf),
            pltpu.VMEM((2, ff, width), bf),
            pltpu.VMEM((pair, ff), bf),
            pltpu.VMEM((line, 2, pair, width), bf),
            pltpu.VMEM((experts, plane * rows), f32),
            pltpu.VMEM((plane, plane, 2, rows), f32),
            pltpu.VMEM((2 * dp, 2, experts, cols), f32),
            pltpu.VMEM((2, ff, width), bf),
            pltpu.VMEM((2, rows, ff), bf),
            pltpu.VMEM((plane, 2, rows), f32),
            dma((2 * plane, 3)), dma((2 * plane,)), dma((2 * plane, 3)), dma((2 * plane,)),
            dma((plane,)), dma((plane,)), dma((plane,)), dma((plane,)),
            dma((3,)), dma((3,)), dma((2 * dp,)), dma((2 * dp,)), dma((plane,)), dma((plane,)),
            dma((CHUNKS,)), dma((CHUNKS,)), dma((CHUNKS,)), dma((CHUNKS,)),
            dma((dp * CHUNKS,)), dma((dp * CHUNKS,)), dma((1,)), dma((1,)), dma((7,)),
        ],
        compiler_params=pltpu.CompilerParams(
            collective_id=0, has_side_effects=True, vmem_limit_bytes=60 * 2**20),
    )(tokens, grad_out, router_weight.T, expert_index.T, w_gate, w_up, w_down)
    def finish(a, b, x, y):
        x[...] = a[...]
        y[...] = b[...]
    gg = pltpu.with_memory_space_constraint(gg, pltpu.VMEM)
    rg = pltpu.with_memory_space_constraint(rg, pltpu.VMEM)
    gg, rg = pl.pallas_call(
        finish,
        out_shape=(jax.ShapeDtypeStruct((top, rows), f32), jax.ShapeDtypeStruct((experts, cols), f32)),
        in_specs=[vmem, vmem],
        out_specs=(vmem, vmem),
    )(gg, rg)
    return gg.T, rg.T


def solution(mesh):
    n, dp = mesh.shape["expert"], mesh.shape["dp"]

    def on_device(tokens, grad_out, router_weight, expert_index, w_gate, w_up, w_down):
        rows, width = tokens.shape
        ff = w_gate.shape[2]
        held = 2 * (2 * n // 2 * rows * width * 2 + 8 * ff * width)
        fits = n % 4 == 0 and n // 4 == 4 and dp == 2 and held < 44 * 2**20 and width % (128 * n) == 0
        fits = fits and ff % (16 * dp * CHUNKS) == 0 and ff % 128 == 0
        fits = fits and rows % 128 == 0 and router_weight.shape[1] == n
        body = functools.partial(fused, n, dp) if fits else plain
        return body(tokens, grad_out, router_weight, expert_index, w_gate, w_up, w_down)

    in_specs = (
        P(("dp", "expert"), None),
        P(("dp", "expert"), None),
        P(),
        P(("dp", "expert"), None),
        P("expert", None, None),
        P("expert", None, None),
        P("expert", None, None),
    )
    out_specs = (P(("dp", "expert"), None), P("expert", None))
    return jax.shard_map(
        on_device, mesh=mesh, in_specs=in_specs, out_specs=out_specs, check_vma=False
    )
```

time: 98.6 us -> 91.9 us (0.932)
  Pallas kernels: 97.8 us -> 91.1 us
    pallas_call x1, Pallas kernels: 97.2 us -> 90.5 us  [fused(): pl.pallas_call(functools.partial(layer_kernel, n, dp), out_shape=(pltpu.V...]
where the time goes in v2:
time: 91.9 us; the launch traced here: 91.7 us
  Pallas kernels  91.1 us (99%)
    pallas_call x1, Pallas kernels, fused(): pl.pallas_call(functools.partial(layer_kernel, n, dp), out_shape=(pltpu.V...  90.5 us

profile of v2, /device:TPU:0, one launch (start us, length us, event | category | flops | bytes accessed | tf_op | source)
XLA Modules:
  0.0 91.7 jit_solution(1187345959989844448)
XLA Ops:
  0.6 90.5 %shard_map.86 = (f32[8,128]{1,0:T(8,128)S(1)}, f32[16,128]{1,0:T(8,128)S(1)}) custom-call(bf16[128,2048]{1,0:T(8,128)(2,1)} %tok_in.1, bf16[128,2048]{1,0:T(8,128)(2,1)} %grad_in.1, bf16[16,2048]{1,0:T(8,128)(2,1)} %bitcast.4, s32[8,128]{1,0:T(8,128)} %bitcast.5, bf16[1,2048,768]{2,1,0:T(8,128)(2,1)} %wg_in.1, bf16[1,2048,768]{2,1,0:T(8,128)(2,1)} %wu_in.1, ...), custom_call_target="tpu_custom_call" | custom-call | tf_op jit(solution)/shard_map/pallas_call | solution.py:427
  91.1 0.6 shard_map.87

commit v3 on v2

--- a/solution.py
+++ b/solution.py
@@ -54,54 +54,56 @@
               ("S", "g", 3, 0, 0, IN), ("S", "g", 3, 0, 1, IN), ("send_down",)],
     "p0": [("F", "x", 2, 0, 0, SIDE), ("F", "x", 2, 0, 1, SIDE), ("W", "x", 3, 1, 0), ("W", "x", 3, 1, 1)],
     "p1": [("F", "x", 1, 0, 0, SIDE)],
-    "p2": [("send_hidden",), ("F", "x", 1, 0, 1, SIDE), ("W", "x", 2, 1, 0), ("W", "x", 2, 1, 1)],
+    "p2": [("send_hidden", 0), ("F", "x", 1, 0, 1, SIDE), ("W", "x", 2, 1, 0), ("W", "x", 2, 1, 1)],
     "p3": [("F", "x", 0, 0, 0, SIDE)],
-    "p4": [("F", "x", 0, 0, 1, SIDE), ("W", "x", 1, 1, 0), ("W", "x", 1, 1, 1)],
-    "p5": [("F", "g", 2, 0, 1, SIDE)],
-    "p6": [("F", "g", 1, 0, 0, SIDE), ("W", "x", 0, 1, 0), ("W", "x", 0, 1, 1)],
-    "p7": [],
-    "r0": [("F", "g", 1, 0, 1, SIDE)],
-    "r1": [("F", "g", 0, 0, 0, SIDE)],
+    "p4": [("send_hidden", 1), ("F", "x", 0, 0, 1, SIDE), ("W", "x", 1, 1, 0), ("W", "x", 1, 1, 1)],
+    "p5": [("F", "g", 1, 0, 0, SIDE)],
+    "r0": [],
+    "r1": [("F", "g", 1, 0, 1, SIDE)],
+    "p6": [("W", "x", 0, 1, 0), ("W", "x", 0, 1, 1)],
+    "p7": [("F", "g", 0, 0, 0, SIDE)],
     "r2": [("F", "g", 0, 0, 1, SIDE)],
     "r3": [("W", "g", 1, 1, 0), ("W", "g", 1, 1, 1)],
-    "r4": [("W", "g", 2, 0, 0)],
-    "r5": [("W", "g", 2, 1, 1), ("W", "g", 2, 1, 0)],
-    "r6": [("W", "g", 0, 1, 0), ("W", "g", 0, 1, 1)],
+    "r4": [("wait_rest",)],
+    "r5": [("W", "g", 0, 1, 0), ("W", "g", 0, 1, 1)],
+    "r6": [("W", "g", 2, 1, 0), ("W", "g", 2, 1, 1)],
     "r7": [],
+    "last": [],
 }
 NEXT = {
     "start": [("S", "x", 2, 0, 0, OUT, IN, SIDE), ("S", "x", 2, 0, 1, OUT, IN, SIDE)],
     "p0": [("F", "x", 3, 0, 0, IN, SIDE), ("F", "x", 1, 0, 0, OUT, SIDE),
            ("F", "x", 3, 0, 1, IN, SIDE), ("F", "x", 1, 0, 1, OUT, SIDE),
-           ("S", "g", 2, 0, 0, IN, SIDE), ("W", "x", 2, 1, 0), ("W", "x", 2, 1, 1)],
-    "p1": [("F", "x", 0, 0, 0, OUT, SIDE), ("F", "g", 3, 0, 0, IN, SIDE)],
-    "p2": [("F", "x", 0, 0, 1, OUT, SIDE), ("F", "g", 3, 0, 1, IN, SIDE), ("S", "g", 2, 0, 1, OUT, IN, SIDE),
-           ("W", "x", 3, 1, 0), ("W", "x", 3, 1, 1)],
-    "p3": [("F", "g", 1, 0, 0, OUT), ("pass_down", 0)],
-    "p4": [("W", "x", 1, 1, 0), ("W", "x", 1, 1, 1)],
-    "p5": [("pass_down", 1), ("F", "g", 2, 1, 0, IN)],
-    "p6": [("F", "g", 1, 0, 1, OUT, SIDE), ("cross_down", 0), ("F", "g", 0, 0, 0, OUT), ("pass_down", 2),
-           ("F", "g", 3, 1, 0, IN), ("cross_down", 1), ("F", "g", 0, 0, 1, OUT), ("S", "g", 2, 0, 0, OUT),
-           ("P", "g", 2, 1, 0, OUT), ("W", "x", 0, 1, 0), ("W", "x", 0, 1, 1)],
-    "p7": [("pass_down", 3), ("cross_down", 2)],
-    "r0": [("F", "g", 3, 1, 1, IN)],
-    "r1": [],
-    "r2": [],
-    "r3": [("cross_down", 3)],
-    "r4": [("help",)],
-    "r5": [("W", "g", 0, 1, 0), ("W", "g", 0, 1, 1)],
-    "r6": [("W", "g", 2, 1, 1)],
+           ("S", "g", 2, 0, 0, IN, SIDE), ("S", "g", 2, 0, 1, IN), ("W", "x", 2, 1, 0), ("W", "x", 2, 1, 1)],
+    "p1": [("F", "g", 3, 0, 0, IN, SIDE), ("F", "x", 0, 0, 0, OUT, SIDE)],
+    "p2": [("F", "x", 0, 0, 1, OUT), ("send_rest",), ("F", "g", 3, 0, 1, IN, SIDE), ("S", "g", 2, 0, 1, SIDE),
+           ("W", "x", 3, 1, 0), ("F", "x", 3, 1, 1, IN), ("F", "g", 1, 0, 0, OUT), ("pass_down", 0)],
+    "p3": [("pass_down", 1)],
+    "p4": [("W", "x", 1, 1, 0), ("W", "x", 1, 1, 1), ("F", "g", 1, 0, 1, OUT, SIDE)],
+    "p5": [("F", "g", 0, 0, 0, OUT), ("F", "g", 2, 1, 0, IN), ("pass_down", 2), ("cross_down", 0)],
+    "r0": [("F", "g", 0, 0, 1, OUT), ("P", "g", 2, 1, 0, OUT), ("pass_down", 3), ("cross_down", 1)],
+    "r1": [("F", "g", 3, 1, 0, IN)],
+    "p6": [("pass_down", 4), ("W", "x", 0, 1, 1), ("W", "x", 0, 1, 0)],
+    "p7": [("pass_down", 5), ("cross_down", 2)],
+    "r2": [("F", "g", 3, 1, 1, IN), ("cross_down", 3), ("F", "g", 2, 1, 1, OUT)],
+    "r3": [("cross_down", 4)],
+    "r4": [],
+    "r5": [],
+    "r6": [("cross_down", 5), ("help", 0), ("W", "g", 0, 1, 0), ("W", "g", 0, 1, 1)],
     "r7": [("W", "g", 1, 1, 0), ("W", "g", 1, 1, 1)],
+    "last": [("help", 1)],
 }
 BLOCKS = [((3, 0), (2, 0)), ((1, 0), (3, 0)), ((0, 0), (1, 0)), ((1, 1), (0, 0)),
-          ((2, 0), (3, 1)), ((2, 1), (0, 1)), ((0, 1), (2, 1)), ((0, 1), (1, 1))]
-CHUNKS = 4
+          ((2, 0), (3, 1)), ((0, 1), (2, 1)), ((2, 1), (0, 1)), ((2, 1), (1, 1))]
+EARLY = 2
+CHUNKS = 6
+KEPT = 6
 
 
 def layer_kernel(n, dp, tok_in, grad_in, rw_in, idx_in, wg_in, wu_in, wd_in, gg_out, rg_out,
-                 tok, grad, rw, idx, wg, wu, wd, hid, eo, lg, dots, part, far_wd, sent, extra,
-                 s_x, r_x, s_g, r_g, s_i, r_i, s_d, r_d, s_w, r_w, s_p, r_p, s_e, r_e,
-                 s_f, r_f, s_fx, r_fx, s_fc, r_fc, s_h, r_h, loc):
+                 tok, grad, rw, idx, wg, wu, wd, hid, eo, lg, dots, part, far_wd, sent, more,
+                 s_way, r_x, r_g, s_i, r_i, s_d, r_d, s_w, r_w, s_p, r_p,
+                 s_f, r_f, s_fx, r_fx, s_fc, r_fc, s_h, r_h, s_t, r_t, loc):
     plane = n // 2
     line = plane // 2
     me = lax.axis_index("expert")
@@ -141,15 +143,14 @@
             return dev(z - step, y, c)
         return dev(z, 1 - y, c)
 
-    kinds = {"x": (tok, tok_in, s_x, r_x), "g": (grad, grad_in, s_g, r_g)}
-
-    def piece(kind, m, f, part_of, way, mine=False):
-        buf, inp, ss, rs = kinds[kind]
+    kinds = {"x": (tok, r_x), "g": (grad, r_g)}
+
+    def piece(kind, m, f, part_of, way):
+        buf, rs = kinds[kind]
         zb, yb = real(m), side(f)
         at = buf.at[zb, pl.ds(pl.multiple_of(yb * rows + part_of * half, 16), half)]
-        src = inp.at[pl.ds(part_of * half, half)] if mine else at
         slot = (zb * 2 + yb) * 2 + part_of
-        return remote(src, at, ss.at[slot, way], rs.at[slot], target(way))
+        return remote(at, at, s_way.at[way], rs.at[slot], target(way))
 
     twin = {"dp": (xd + 1) % dp}
     mate = {"expert": q * 2 + (1 - c)}
@@ -160,18 +161,26 @@
 
     def down(k):
         at = down_rows(xd, k)
-        return remote(wd_in.at[0, at], far_wd.at[c, at], s_f.at[k], r_f.at[k], target(IN))
+        return remote(wd_in.at[0, at], far_wd.at[c, at], s_f.at[0], r_f.at[k], target(IN))
 
     def down_twin(k):
         at = far_wd.at[c, down_rows(xd, k)]
-        return remote(at, at, s_fx.at[k], r_fx.at[k], twin)
+        return remote(at, at, s_fx.at[0], r_fx.at[k], twin)
 
     def down_mate(other, k):
         at = far_wd.at[c, down_rows((xd + other) % dp, k)]
-        return remote(at, at, s_fc.at[other * CHUNKS + k], r_fc.at[other * CHUNKS + k], mate)
-
-    def hidden_send():
-        return remote(sent, sent, s_h.at[0], r_h.at[0], target(IN))
+        return remote(at, at, s_fc.at[0], r_fc.at[0], mate)
+
+    fewer = more.shape[1]
+    rest = rows - fewer
+
+    def hidden_send(which, r):
+        buf = more if which else sent
+        return remote(buf.at[r], buf.at[r], s_h.at[2 * which + r], r_h.at[2 * which + r], target(IN))
+
+    def rest_send(way):
+        at = grad.at[real(line - 2), pl.ds(pl.multiple_of(y * rows + fewer, 16), rest)]
+        return remote(at, at, s_t.at[0], r_t.at[0], target(way))
 
     def plane_dev(k):
         return {"expert": ((q + k) % plane) * 2 + c}
@@ -179,9 +188,8 @@
     def owner_dev(k):
         return {"dp": (xd + k // 2) % dp, "expert": q * 2 + (c + k) % 2}
 
-    at_end = real(line - 1) * 2 + y
-    extra_sends = [remote(extra.at[at_end], extra.at[at_end], s_e.at[k], r_e.at[at_end], plane_dev(k))
-                   for k in range(1, plane)]
+    def few(buf, k, ss, rs):
+        return remote(buf.at[pl.ds(0, k)], buf.at[pl.ds(0, k)], ss, rs, plane_dev(1))
 
     def block_dots(left, right):
         total = jnp.zeros((rows, 128), jnp.float32)
@@ -191,26 +199,29 @@
 
     dt = width // 4 if width % 512 == 0 else width
 
-    def help_end():
-        hidden_send().wait_recv()
-        for k in range(CHUNKS):
-            down_mate(0, k).wait_recv()
-            down_mate(1, k).wait_recv()
-        theirs = pl.ds(pl.multiple_of((1 - y) * rows, 16), rows)
+    def help_end(which):
+        if which == 0:
+            remote(far_wd.at[0], far_wd.at[0], s_fc.at[0], r_fc.at[0], mate).wait_recv()
+        buf = more if which else sent
+        count = buf.shape[1]
+        zb, base = (real(line - 2), y * rows) if which else (real(line - 1), (1 - y) * rows)
+        theirs = pl.ds(pl.multiple_of(base, 16), count)
 
         @pl.loop(0, 2)
         def _(r):
-            total = jnp.zeros((rows, 128), jnp.float32)
+            hidden_send(which, r).wait_recv()
+            total = jnp.zeros((count, 128), jnp.float32)
             for j in range(width // dt):
-                got = jnp.dot(sent[r], far_wd[r, :, j * dt:(j + 1) * dt],
+                got = jnp.dot(buf[r], far_wd[r, :, j * dt:(j + 1) * dt],
                               preferred_element_type=jnp.float32).astype(jnp.bfloat16).astype(jnp.float32)
                 for i in range(dt // 128):
                     lo = j * dt + i * 128
                     total += got[:, i * 128:(i + 1) * 128] * grad[
-                        real(line - 1), theirs, lo:lo + 128].astype(jnp.float32)
-            extra[at_end, pl.ds(r, 1), :] = jnp.sum(total.T, axis=0, keepdims=True)
-        for w in extra_sends:
-            w.start()
+                        zb, theirs, lo:lo + 128].astype(jnp.float32)
+            row = jnp.sum(total.T, axis=0, keepdims=True)
+            if count < rows:
+                row = jnp.concatenate([row, jnp.zeros((1, rows - count), jnp.float32)], axis=1)
+            dots[q, plane + which, pl.ds(r, 1), :] = row
 
     def run(ops):
         for op in ops:
@@ -218,7 +229,14 @@
                 for k in range(CHUNKS):
                     down(k).start()
             elif op[0] == "send_hidden":
-                hidden_send().start()
+                hidden_send(op[1], 0).start()
+                hidden_send(op[1], 1).start()
+            elif op[0] == "send_rest":
+                if rest:
+                    rest_send(OUT).start()
+            elif op[0] == "wait_rest":
+                if rest:
+                    rest_send(SIDE).wait_recv()
             elif op[0] == "pass_down":
                 down(op[1]).wait_recv()
                 down_twin(op[1]).start()
@@ -227,13 +245,13 @@
                 down_twin(op[1]).wait_recv()
                 down_mate(1, op[1]).start()
             elif op[0] == "help":
-                help_end()
+                help_end(op[1])
             else:
                 what, kind, m, f, part_of = op[:5]
                 if what in "FW":
                     piece(kind, m, f, part_of, SIDE).wait_recv()
                 for way in op[5:]:
-                    piece(kind, m, f, part_of, way, mine=what == "S").start()
+                    piece(kind, m, f, part_of, way).start()
 
     def slot(name):
         if END[name]:
@@ -242,24 +260,22 @@
             pl.when(end == 0)(lambda: run(NEXT[name]))
 
     def sent_all(table):
-        for ops in table.values():
-            for op in ops:
-                if op[0] == "send_down":
-                    for k in range(CHUNKS):
-                        down(k).wait_send()
-                elif op[0] == "send_hidden":
-                    hidden_send().wait_send()
-                elif op[0] == "pass_down":
-                    down_twin(op[1]).wait_send()
-                    down_mate(0, op[1]).wait_send()
-                elif op[0] == "cross_down":
-                    down_mate(1, op[1]).wait_send()
-                elif op[0] == "help":
-                    for w in extra_sends:
-                        w.wait_send()
-                else:
-                    for way in op[5:]:
-                        piece(op[1], op[2], op[3], op[4], way).wait_send()
+        ways = [way for ops in table.values() for op in ops if op[0] in ("S", "F", "P") for way in op[5:]]
+        for way in range(3):
+            if way in ways:
+                at = tok.at[:, pl.ds(0, ways.count(way) * half // line)]
+                remote(at, at, s_way.at[way], r_x.at[0], target(SIDE)).wait_send()
+        if table is END:
+            at = far_wd.at[0, pl.ds(0, ff // dp)]
+            remote(at, at, s_f.at[0], r_f.at[0], target(IN)).wait_send()
+            for k in range(4):
+                hidden_send(k // 2, k % 2).wait_send()
+            return
+        at = far_wd.at[0, pl.ds(0, ff // dp)]
+        remote(at, at, s_fx.at[0], r_fx.at[0], twin).wait_send()
+        remote(far_wd.at[0], far_wd.at[0], s_fc.at[0], r_fc.at[0], mate).wait_send()
+        if rest:
+            rest_send(OUT).wait_send()
 
     barrier = pltpu.get_barrier_semaphore()
 
@@ -279,18 +295,22 @@
              pltpu.make_async_copy(wu_in.at[0], wu.at[c], loc.at[4]),
              pltpu.make_async_copy(wd_in.at[0], wd.at[c], loc.at[5]),
              pltpu.make_async_copy(rw_in, rw, loc.at[6])]
-    for copy in local:
+    for copy in local[:2]:
         copy.start()
     pl.when(end == 0)(lambda: pl.semaphore_wait(barrier, 2 + 2 * dp))
     pl.when(end == 1)(lambda: pl.semaphore_wait(barrier, 1 + 2 * dp))
 
+    for copy in local[:2]:
+        copy.wait()
     slot("start")
+    for copy in local[2:]:
+        copy.start()
     weights = [remote(wg_in.at[0], wg.at[c], s_w.at[0], r_w.at[0], mate),
                remote(wu_in.at[0], wu.at[c], s_w.at[1], r_w.at[1], mate),
                remote(wd_in.at[0], wd.at[c], s_w.at[2], r_w.at[2], mate)]
     for w in weights:
         w.start()
-    index_sends = [remote(idx_in, idx.at[q], s_i.at[k], r_i.at[k], plane_dev(k)) for k in range(1, plane)]
+    index_sends = [remote(idx_in, idx.at[q], s_i.at[0], r_i.at[0], plane_dev(k)) for k in range(1, plane)]
 
     ft = ff // 3 if ff % 384 == 0 else ff
 
@@ -303,10 +323,14 @@
             u = jnp.dot(x, wu[r, :, at], preferred_element_type=jnp.float32)
             hid[:, at] = (g / (1.0 + jnp.exp(-g)) * u).astype(jnp.bfloat16)
 
-        if keep:
+        if keep == 0:
             @pl.when(end == 1)
             def _():
                 sent[r] = hid[pl.ds(pl.multiple_of((1 - y) * rows, 16), rows), :]
+        if keep == 1:
+            @pl.when(end == 1)
+            def _():
+                more[r] = hid[pl.ds(pl.multiple_of(y * rows, 16), fewer), :]
 
         @pl.loop(0, width // dt)
         def _(j):
@@ -317,21 +341,6 @@
             lg[:, pl.ds(pl.multiple_of(zp * pair, 128), pair)] = lax.dot_general(
                 rw[...], tok[zp], (((1,), (1,)), ((), ())), preferred_element_type=jnp.float32)
 
-    order = [2 + end, 3 - end, 1, 0]
-    for i in range(line):
-        for k in range(2):
-            slot("p" + str(2 * i + k))
-            if i == 0 and k == 0:
-                for copy in local:
-                    copy.wait()
-            if i == 0 and k == 1:
-                for w in weights:
-                    w.wait_recv()
-            produce(real(order[i]), c + k - 2 * c * k, k == 0, i == 0)
-
-    for w in index_sends:
-        w.start()
-
     def reduce_block(zb, yb):
         at = pl.ds(pl.multiple_of(yb * rows, 16), rows)
 
@@ -341,20 +350,41 @@
                              lambda j: grad[zb, at, j * 128:(j + 1) * 128])
             dots[q, zb * 2 + yb, pl.ds(r, 1), :] = row
 
-    for i, (a, b) in enumerate(BLOCKS):
-        slot("r" + str(i))
-        m = end * a[0] + (1 - end) * b[0]
-        f = end * a[1] + (1 - end) * b[1]
-        if i < len(BLOCKS) - 1:
-            reduce_block(real(m), side(f))
-        else:
-            pl.when(end == 0)(lambda: reduce_block(real(m), side(f)))
-
-    dot_sends = [remote(dots.at[q], dots.at[q], s_d.at[k], r_d.at[k], plane_dev(k)) for k in range(1, plane)]
+    def reduce_some(lo, hi):
+        for i in range(lo, hi):
+            slot("r" + str(i))
+            a, b = BLOCKS[i]
+            m = end * a[0] + (1 - end) * b[0]
+            f = end * a[1] + (1 - end) * b[1]
+            if a != BLOCKS[i - 1][0] and (rest or a != (2, 0)):
+                reduce_block(real(m), side(f))
+            else:
+                pl.when(end == 0)(lambda: reduce_block(real(m), side(f)))
+
+    order = [2 + end, 3 - end, 1, 0]
+    for i in range(line):
+        if i == line - 1:
+            reduce_some(0, EARLY)
+        for k in range(2):
+            slot("p" + str(2 * i + k))
+            if i == 0 and k == 0:
+                for copy in local[2:]:
+                    copy.wait()
+            if i == 0 and k == 1:
+                for w in weights:
+                    w.wait_recv()
+            produce(real(order[i]), c + k - 2 * c * k, k == 0, i)
+
+    for w in index_sends:
+        w.start()
+
+    reduce_some(EARLY, len(BLOCKS))
+    slot("last")
+
+    dot_sends = [remote(dots.at[q], dots.at[q], s_d.at[0], r_d.at[0], plane_dev(k)) for k in range(1, plane)]
     for w in dot_sends:
         w.start()
-    for w in index_sends:
-        w.wait()
+    few(idx, plane - 1, s_i.at[0], r_i.at[0]).wait()
     labels = lax.broadcasted_iota(jnp.int32, (experts, plane * rows), 0)
     chosen = jnp.zeros((experts, plane * rows), jnp.float32)
     for k in range(top):
@@ -362,17 +392,22 @@
         chosen = jnp.where(labels == named, 1.0, chosen)
     weight = jnp.where(chosen > 0.0, jnp.exp(jnp.where(chosen > 0.0, lg[...], 0.0)), 0.0)
     gates = weight / jnp.sum(weight, axis=0, keepdims=True)
-    ends = {0: 2, 1: 3, plane - 2: plane - 4, plane - 1: plane - 3}
-    for b, helper in ends.items():
-        pl.when(q != helper)(lambda: remote(
-            extra.at[b], extra.at[b], s_e.at[1], r_e.at[b], plane_dev(1)).wait_recv())
-    for w in dot_sends:
-        w.wait()
+    ends = (0, 1, plane - 2, plane - 1)
+    few(dots, plane - 1, s_d.at[0], r_d.at[0]).wait()
+    lanes = lax.broadcasted_iota(jnp.int32, (2, rows), 1)
+
+    def next_to(b):
+        return b + 2 if b < 2 else b - 2
+
+    def patched(b):
+        helped = dots[next_to(b), plane + 1]
+        return jnp.where(lanes < fewer, helped, dots[b, next_to(b)]) if rest else helped
 
     def dots_of(b):
         blocks = [dots[b, k] for k in range(plane)]
         if b in ends:
-            blocks[b ^ 1] = extra[b]
+            blocks[b ^ 1] = dots[next_to(b), plane]
+            blocks[next_to(b)] = patched(b)
         return jnp.concatenate(blocks, axis=1)
 
     all_dots = jnp.concatenate([dots_of(b) for b in range(plane)], axis=0)
@@ -389,11 +424,16 @@
     terms = split[:experts] + split[experts:]
     part[0, 0] = terms[:, :cols]
     part[0, 1] = terms[:, cols:]
-    part_sends = [remote(part.at[0, (c + k) % 2], part.at[k, 0], s_p.at[k], r_p.at[k], owner_dev(k))
+    part_sends = [remote(part.at[0, (c + k) % 2], part.at[k, 0], s_p.at[0], r_p.at[0], owner_dev(k))
                   for k in range(1, 2 * dp)]
     for w in part_sends:
         w.start()
-    held = [jnp.where(q == (b ^ 1), extra[b], dots[b, q]) if b in ends else dots[b, q] for b in range(plane)]
+    held = []
+    for b in range(plane):
+        row = dots[b, q]
+        if b in ends:
+            row = jnp.where(q == (b ^ 1), dots[next_to(b), plane], jnp.where(q == next_to(b), patched(b), row))
+        held.append(row)
     held = jnp.concatenate(held, axis=0)
     names = idx[q]
     small = lax.broadcasted_iota(jnp.int32, (experts, rows), 0)
@@ -404,8 +444,8 @@
         w.wait_send()
     pl.when(end == 1)(lambda: sent_all(END))
     pl.when(end == 0)(lambda: sent_all(NEXT))
-    for w in part_sends:
-        w.wait()
+    at = part.at[pl.ds(0, 2 * dp - 1), 0]
+    remote(at, at, s_p.at[0], r_p.at[0], mate).wait()
     total = part[0, c]
     for k in range(1, 2 * dp):
         total += part[k, 0]
@@ -440,16 +480,15 @@
             pltpu.VMEM((pair, ff), bf),
             pltpu.VMEM((line, 2, pair, width), bf),
             pltpu.VMEM((experts, plane * rows), f32),
-            pltpu.VMEM((plane, plane, 2, rows), f32),
+            pltpu.VMEM((plane, plane + 2, 2, rows), f32),
             pltpu.VMEM((2 * dp, 2, experts, cols), f32),
             pltpu.VMEM((2, ff, width), bf),
             pltpu.VMEM((2, rows, ff), bf),
-            pltpu.VMEM((plane, 2, rows), f32),
-            dma((2 * plane, 3)), dma((2 * plane,)), dma((2 * plane, 3)), dma((2 * plane,)),
-            dma((plane,)), dma((plane,)), dma((plane,)), dma((plane,)),
-            dma((3,)), dma((3,)), dma((2 * dp,)), dma((2 * dp,)), dma((plane,)), dma((plane,)),
-            dma((CHUNKS,)), dma((CHUNKS,)), dma((CHUNKS,)), dma((CHUNKS,)),
-            dma((dp * CHUNKS,)), dma((dp * CHUNKS,)), dma((1,)), dma((1,)), dma((7,)),
+            pltpu.VMEM((2, rows * KEPT // 8, ff), bf),
+            dma((3,)), dma((2 * plane,)), dma((2 * plane,)),
+            dma((1,)), dma((1,)), dma((1,)), dma((1,)), dma((3,)), dma((3,)), dma((1,)), dma((1,)),
+            dma((1,)), dma((CHUNKS,)), dma((1,)), dma((CHUNKS,)), dma((1,)), dma((1,)),
+            dma((4,)), dma((4,)), dma((1,)), dma((1,)), dma((7,)),
         ],
         compiler_params=pltpu.CompilerParams(
             collective_id=0, has_side_effects=True, vmem_limit_bytes=60 * 2**20),

time: 91.9 us -> 87.6 us (0.953)
  Pallas kernels: 91.1 us -> 86.8 us
    pallas_call x1, Pallas kernels: 90.5 us -> 86.2 us  [fused(): pl.pallas_call(functools.partial(layer_kernel, n, dp), out_shape=(pltpu.V...]
where the time goes in v3:
time: 87.6 us; the launch traced here: 87.5 us
  Pallas kernels  86.8 us (99%)
    pallas_call x1, Pallas kernels, fused(): pl.pallas_call(functools.partial(layer_kernel, n, dp), out_shape=(pltpu.V...  86.2 us

profile of v3, /device:TPU:0, one launch (start us, length us, event | category | flops | bytes accessed | tf_op | source)
XLA Modules:
  0.0 87.5 jit_solution(10716854250639008052)
XLA Ops:
  0.6 86.2 %shard_map.86 = (f32[8,128]{1,0:T(8,128)S(1)}, f32[16,128]{1,0:T(8,128)S(1)}) custom-call(bf16[128,2048]{1,0:T(8,128)(2,1)} %tok_in.1, bf16[128,2048]{1,0:T(8,128)(2,1)} %grad_in.1, bf16[16,2048]{1,0:T(8,128)(2,1)} %bitcast.4, s32[8,128]{1,0:T(8,128)} %bitcast.5, bf16[1,2048,768]{2,1,0:T(8,128)(2,1)} %wg_in.1, bf16[1,2048,768]{2,1,0:T(8,128)(2,1)} %wu_in.1, ...), custom_call_target="tpu_custom_call" | custom-call | tf_op jit(solution)/shard_map/pallas_call | solution.py:467
  86.9 0.6 shard_map.87

commit v4 on v3

--- a/solution.py
+++ b/solution.py
@@ -57,17 +57,17 @@
     "p2": [("send_hidden", 0), ("F", "x", 1, 0, 1, SIDE), ("W", "x", 2, 1, 0), ("W", "x", 2, 1, 1)],
     "p3": [("F", "x", 0, 0, 0, SIDE)],
     "p4": [("send_hidden", 1), ("F", "x", 0, 0, 1, SIDE), ("W", "x", 1, 1, 0), ("W", "x", 1, 1, 1)],
-    "p5": [("F", "g", 1, 0, 0, SIDE)],
+    "p5": [("send_rest", 0), ("F", "g", 1, 0, 0, SIDE)],
     "r0": [],
     "r1": [("F", "g", 1, 0, 1, SIDE)],
     "p6": [("W", "x", 0, 1, 0), ("W", "x", 0, 1, 1)],
     "p7": [("F", "g", 0, 0, 0, SIDE)],
     "r2": [("F", "g", 0, 0, 1, SIDE)],
     "r3": [("W", "g", 1, 1, 0), ("W", "g", 1, 1, 1)],
-    "r4": [("wait_rest",)],
-    "r5": [("W", "g", 0, 1, 0), ("W", "g", 0, 1, 1)],
-    "r6": [("W", "g", 2, 1, 0), ("W", "g", 2, 1, 1)],
-    "r7": [],
+    "r4": [("wait_rest", 1)],
+    "r5": [("wait_rest", 0)],
+    "r6": [("W", "g", 0, 1, 0), ("W", "g", 0, 1, 1)],
+    "r7": [("W", "g", 2, 1, 0), ("W", "g", 2, 1, 1)],
     "last": [],
 }
 NEXT = {
@@ -76,7 +76,7 @@
            ("F", "x", 3, 0, 1, IN, SIDE), ("F", "x", 1, 0, 1, OUT, SIDE),
            ("S", "g", 2, 0, 0, IN, SIDE), ("S", "g", 2, 0, 1, IN), ("W", "x", 2, 1, 0), ("W", "x", 2, 1, 1)],
     "p1": [("F", "g", 3, 0, 0, IN, SIDE), ("F", "x", 0, 0, 0, OUT, SIDE)],
-    "p2": [("F", "x", 0, 0, 1, OUT), ("send_rest",), ("F", "g", 3, 0, 1, IN, SIDE), ("S", "g", 2, 0, 1, SIDE),
+    "p2": [("F", "x", 0, 0, 1, OUT), ("send_rest", 1), ("F", "g", 3, 0, 1, IN, SIDE), ("S", "g", 2, 0, 1, SIDE),
            ("W", "x", 3, 1, 0), ("F", "x", 3, 1, 1, IN), ("F", "g", 1, 0, 0, OUT), ("pass_down", 0)],
     "p3": [("pass_down", 1)],
     "p4": [("W", "x", 1, 1, 0), ("W", "x", 1, 1, 1), ("F", "g", 1, 0, 1, OUT, SIDE)],
@@ -94,10 +94,10 @@
     "last": [("help", 1)],
 }
 BLOCKS = [((3, 0), (2, 0)), ((1, 0), (3, 0)), ((0, 0), (1, 0)), ((1, 1), (0, 0)),
-          ((2, 0), (3, 1)), ((0, 1), (2, 1)), ((2, 1), (0, 1)), ((2, 1), (1, 1))]
+          ((2, 0), (3, 1)), ((3, 1), (2, 1)), ((0, 1), (0, 1)), ((2, 1), (1, 1))]
 EARLY = 2
 CHUNKS = 6
-KEPT = 6
+KEPT = (6, 6)
 
 
 def layer_kernel(n, dp, tok_in, grad_in, rw_in, idx_in, wg_in, wu_in, wd_in, gg_out, rg_out,
@@ -171,16 +171,16 @@
         at = far_wd.at[c, down_rows((xd + other) % dp, k)]
         return remote(at, at, s_fc.at[0], r_fc.at[0], mate)
 
-    fewer = more.shape[1]
-    rest = rows - fewer
+    fewer = (sent.shape[1], more.shape[1])
+    rest = (rows - fewer[0], rows - fewer[1])
 
     def hidden_send(which, r):
         buf = more if which else sent
         return remote(buf.at[r], buf.at[r], s_h.at[2 * which + r], r_h.at[2 * which + r], target(IN))
 
-    def rest_send(way):
-        at = grad.at[real(line - 2), pl.ds(pl.multiple_of(y * rows + fewer, 16), rest)]
-        return remote(at, at, s_t.at[0], r_t.at[0], target(way))
+    def rest_send(which, f, way):
+        at = grad.at[real(line - 1 - which), pl.ds(pl.multiple_of(side(f) * rows + fewer[which], 16), rest[which])]
+        return remote(at, at, s_t.at[which], r_t.at[which], target(way))
 
     def plane_dev(k):
         return {"expert": ((q + k) % plane) * 2 + c}
@@ -232,11 +232,11 @@
                 hidden_send(op[1], 0).start()
                 hidden_send(op[1], 1).start()
             elif op[0] == "send_rest":
-                if rest:
-                    rest_send(OUT).start()
+                if rest[op[1]]:
+                    rest_send(op[1], 0, OUT if op[1] else SIDE).start()
             elif op[0] == "wait_rest":
-                if rest:
-                    rest_send(SIDE).wait_recv()
+                if rest[op[1]]:
+                    rest_send(op[1], 1 - op[1], SIDE).wait_recv()
             elif op[0] == "pass_down":
                 down(op[1]).wait_recv()
                 down_twin(op[1]).start()
@@ -270,12 +270,14 @@
             remote(at, at, s_f.at[0], r_f.at[0], target(IN)).wait_send()
             for k in range(4):
                 hidden_send(k // 2, k % 2).wait_send()
+            if rest[0]:
+                rest_send(0, 0, SIDE).wait_send()
             return
         at = far_wd.at[0, pl.ds(0, ff // dp)]
         remote(at, at, s_fx.at[0], r_fx.at[0], twin).wait_send()
         remote(far_wd.at[0], far_wd.at[0], s_fc.at[0], r_fc.at[0], mate).wait_send()
-        if rest:
-            rest_send(OUT).wait_send()
+        if rest[1]:
+            rest_send(1, 0, OUT).wait_send()
 
     barrier = pltpu.get_barrier_semaphore()
 
@@ -326,11 +328,11 @@
         if keep == 0:
             @pl.when(end == 1)
             def _():
-                sent[r] = hid[pl.ds(pl.multiple_of((1 - y) * rows, 16), rows), :]
+                sent[r] = hid[pl.ds(pl.multiple_of((1 - y) * rows, 16), fewer[0]), :]
         if keep == 1:
             @pl.when(end == 1)
             def _():
-                more[r] = hid[pl.ds(pl.multiple_of(y * rows, 16), fewer), :]
+                more[r] = hid[pl.ds(pl.multiple_of(y * rows, 16), fewer[1]), :]
 
         @pl.loop(0, width // dt)
         def _(j):
@@ -356,7 +358,7 @@
             a, b = BLOCKS[i]
             m = end * a[0] + (1 - end) * b[0]
             f = end * a[1] + (1 - end) * b[1]
-            if a != BLOCKS[i - 1][0] and (rest or a != (2, 0)):
+            if (rest[0] or a != (3, 1)) and (rest[1] or a != (2, 0)):
                 reduce_block(real(m), side(f))
             else:
                 pl.when(end == 0)(lambda: reduce_block(real(m), side(f)))
@@ -399,15 +401,16 @@
     def next_to(b):
         return b + 2 if b < 2 else b - 2
 
-    def patched(b):
-        helped = dots[next_to(b), plane + 1]
-        return jnp.where(lanes < fewer, helped, dots[b, next_to(b)]) if rest else helped
+    def patched(b, which):
+        helped = dots[next_to(b), plane + which]
+        mine_at = next_to(b) if which else b ^ 1
+        return jnp.where(lanes < fewer[which], helped, dots[b, mine_at]) if rest[which] else helped
 
     def dots_of(b):
         blocks = [dots[b, k] for k in range(plane)]
         if b in ends:
-            blocks[b ^ 1] = dots[next_to(b), plane]
-            blocks[next_to(b)] = patched(b)
+            blocks[b ^ 1] = patched(b, 0)
+            blocks[next_to(b)] = patched(b, 1)
         return jnp.concatenate(blocks, axis=1)
 
     all_dots = jnp.concatenate([dots_of(b) for b in range(plane)], axis=0)
@@ -432,7 +435,7 @@
     for b in range(plane):
         row = dots[b, q]
         if b in ends:
-            row = jnp.where(q == (b ^ 1), dots[next_to(b), plane], jnp.where(q == next_to(b), patched(b), row))
+            row = jnp.where(q == (b ^ 1), patched(b, 0), jnp.where(q == next_to(b), patched(b, 1), row))
         held.append(row)
     held = jnp.concatenate(held, axis=0)
     names = idx[q]
@@ -483,12 +486,12 @@
             pltpu.VMEM((plane, plane + 2, 2, rows), f32),
             pltpu.VMEM((2 * dp, 2, experts, cols), f32),
             pltpu.VMEM((2, ff, width), bf),
-            pltpu.VMEM((2, rows, ff), bf),
-            pltpu.VMEM((2, rows * KEPT // 8, ff), bf),
+            pltpu.VMEM((2, rows * KEPT[0] // 8, ff), bf),
+            pltpu.VMEM((2, rows * KEPT[1] // 8, ff), bf),
             dma((3,)), dma((2 * plane,)), dma((2 * plane,)),
             dma((1,)), dma((1,)), dma((1,)), dma((1,)), dma((3,)), dma((3,)), dma((1,)), dma((1,)),
             dma((1,)), dma((CHUNKS,)), dma((1,)), dma((CHUNKS,)), dma((1,)), dma((1,)),
-            dma((4,)), dma((4,)), dma((1,)), dma((1,)), dma((7,)),
+            dma((4,)), dma((4,)), dma((2,)), dma((2,)), dma((7,)),
         ],
         compiler_params=pltpu.CompilerParams(
             collective_id=0, has_side_effects=True, vmem_limit_bytes=60 * 2**20),

time: 87.6 us -> 87.2 us (level)
  no operation moved by 1% of the time
where the time goes in v4:
time: 87.2 us; the launch traced here: 87 us
  Pallas kernels  86.4 us (99%)
    pallas_call x1, Pallas kernels, fused(): pl.pallas_call(functools.partial(layer_kernel, n, dp), out_shape=(pltpu.V...  85.8 us

profile of v4, /device:TPU:0, one launch (start us, length us, event | category | flops | bytes accessed | tf_op | source)
XLA Modules:
  0.0 87.0 jit_solution(14163811136115060322)
XLA Ops:
  0.6 85.8 %shard_map.86 = (f32[8,128]{1,0:T(8,128)S(1)}, f32[16,128]{1,0:T(8,128)S(1)}) custom-call(bf16[128,2048]{1,0:T(8,128)(2,1)} %tok_in.1, bf16[128,2048]{1,0:T(8,128)(2,1)} %grad_in.1, bf16[16,2048]{1,0:T(8,128)(2,1)} %bitcast.4, s32[8,128]{1,0:T(8,128)} %bitcast.5, bf16[1,2048,768]{2,1,0:T(8,128)(2,1)} %wg_in.1, bf16[1,2048,768]{2,1,0:T(8,128)(2,1)} %wu_in.1, ...), custom_call_target="tpu_custom_call" | custom-call | tf_op jit(solution)/shard_map/pallas_call | solution.py:470
  86.4 0.6 shard_map.87

commit v5 on v4

--- a/solution.py
+++ b/solution.py
@@ -97,7 +97,7 @@
           ((2, 0), (3, 1)), ((3, 1), (2, 1)), ((0, 1), (0, 1)), ((2, 1), (1, 1))]
 EARLY = 2
 CHUNKS = 6
-KEPT = (6, 6)
+KEPT = (7, 6)
 
 
 def layer_kernel(n, dp, tok_in, grad_in, rw_in, idx_in, wg_in, wu_in, wd_in, gg_out, rg_out,
@@ -383,9 +383,13 @@
     reduce_some(EARLY, len(BLOCKS))
     slot("last")
 
-    dot_sends = [remote(dots.at[q], dots.at[q], s_d.at[0], r_d.at[0], plane_dev(k)) for k in range(1, plane)]
-    for w in dot_sends:
-        w.start()
+    def dot_sends(blocks, which):
+        at = dots.at[q, pl.ds(0, blocks)]
+        for k in range(1, plane):
+            remote(at, at, s_d.at[0], r_d.at[which], plane_dev(k)).start()
+
+    pl.when(end == 1)(lambda: dot_sends(plane, 0))
+    pl.when(end == 0)(lambda: dot_sends(plane + 2, 1))
     few(idx, plane - 1, s_i.at[0], r_i.at[0]).wait()
     labels = lax.broadcasted_iota(jnp.int32, (experts, plane * rows), 0)
     chosen = jnp.zeros((experts, plane * rows), jnp.float32)
@@ -395,7 +399,17 @@
     weight = jnp.where(chosen > 0.0, jnp.exp(jnp.where(chosen > 0.0, lg[...], 0.0)), 0.0)
     gates = weight / jnp.sum(weight, axis=0, keepdims=True)
     ends = (0, 1, plane - 2, plane - 1)
-    few(dots, plane - 1, s_d.at[0], r_d.at[0]).wait()
+
+    def dots_wait(own_blocks, from_ends, from_next):
+        at = dots.at[pl.ds(0, plane - 1), pl.ds(0, own_blocks)]
+        remote(at, at, s_d.at[0], r_d.at[0], mate).wait_send()
+        at = dots.at[pl.ds(0, from_ends), pl.ds(0, plane)]
+        remote(at, at, s_d.at[0], r_d.at[0], mate).wait_recv()
+        at = dots.at[pl.ds(0, from_next), pl.ds(0, plane + 2)]
+        remote(at, at, s_d.at[0], r_d.at[1], mate).wait_recv()
+
+    pl.when(end == 1)(lambda: dots_wait(plane, 3, 4))
+    pl.when(end == 0)(lambda: dots_wait(plane + 2, 4, 3))
     lanes = lax.broadcasted_iota(jnp.int32, (2, rows), 1)
 
     def next_to(b):
@@ -489,7 +503,7 @@
             pltpu.VMEM((2, rows * KEPT[0] // 8, ff), bf),
             pltpu.VMEM((2, rows * KEPT[1] // 8, ff), bf),
             dma((3,)), dma((2 * plane,)), dma((2 * plane,)),
-            dma((1,)), dma((1,)), dma((1,)), dma((1,)), dma((3,)), dma((3,)), dma((1,)), dma((1,)),
+            dma((1,)), dma((1,)), dma((1,)), dma((2,)), dma((3,)), dma((3,)), dma((1,)), dma((1,)),
             dma((1,)), dma((CHUNKS,)), dma((1,)), dma((CHUNKS,)), dma((1,)), dma((1,)),
             dma((4,)), dma((4,)), dma((2,)), dma((2,)), dma((7,)),
         ],

time: 87.2 us -> 86.9 us (level)
  no operation moved by 1% of the time
where the time goes in v5:
time: 86.9 us; the launch traced here: 86.8 us
  Pallas kernels  86.1 us (99%)
    pallas_call x1, Pallas kernels, fused(): pl.pallas_call(functools.partial(layer_kernel, n, dp), out_shape=(pltpu.V...  85.5 us

profile of v5, /device:TPU:0, one launch (start us, length us, event | category | flops | bytes accessed | tf_op | source)
XLA Modules:
  0.0 86.8 jit_solution(2374437934689669812)
XLA Ops:
  0.6 85.5 %shard_map.86 = (f32[8,128]{1,0:T(8,128)S(1)}, f32[16,128]{1,0:T(8,128)S(1)}) custom-call(bf16[128,2048]{1,0:T(8,128)(2,1)} %tok_in.1, bf16[128,2048]{1,0:T(8,128)(2,1)} %grad_in.1, bf16[16,2048]{1,0:T(8,128)(2,1)} %bitcast.4, s32[8,128]{1,0:T(8,128)} %bitcast.5, bf16[1,2048,768]{2,1,0:T(8,128)(2,1)} %wg_in.1, bf16[1,2048,768]{2,1,0:T(8,128)(2,1)} %wu_in.1, ...), custom_call_target="tpu_custom_call" | custom-call | tf_op jit(solution)/shard_map/pallas_call | solution.py:484
  86.2 0.6 shard_map.87
